TPU v7x, 16 devices: a whole 2x2x2 slice. The times are simulated.
16 devices in a mesh: ez: 2 (over z), ey: 2 (over y), ex: 4 (over x, core).
Axes of the slice: x: 2, y: 2, z: 2, core: 2. Of those that a mesh axis runs over, the one named last changes fastest.
Arguments:
- tokens: bfloat16 [4096, 2048], P(('ez', 'ey', 'ex'))
- expert_ids: int32 [4096, 6], P(('ez', 'ey', 'ex'))
- gate_weights: float32 [4096, 6], P(('ez', 'ey', 'ex'))
- w_gate: bfloat16 [64, 2048, 1408], P(('ez', 'ey', 'ex'))
- w_up: bfloat16 [64, 2048, 1408], P(('ez', 'ey', 'ex'))
- w_down: bfloat16 [64, 1408, 2048], P(('ez', 'ey', 'ex'))
Outputs:
- output: bfloat16 [4096, 2048], P(('ez', 'ey', 'ex'))
All inputs are finite; a program needn't handle non-finite values.
Results may differ from a plain program's by a relative error of at most 0.00618276.
Values are sent between devices in bfloat16 or wider.
A program may use at most 1 GiB of HBM per device.

v0:
```python
import math
import jax
import jax.numpy as jnp
from jax import lax
from jax.sharding import PartitionSpec as P


def pack_rows(chosen, gate_vals, per_expert):
    row_rank = jnp.cumsum(chosen.astype(jnp.int32), axis=0) - 1
    slot_idx = jnp.where(chosen, row_rank, per_expert)
    row_idx = jnp.broadcast_to(jnp.arange(chosen.shape[0])[:, None], chosen.shape)
    exp_idx = jnp.broadcast_to(jnp.arange(chosen.shape[1])[None, :], chosen.shape)
    pick_rows = jnp.zeros((chosen.shape[1], per_expert), jnp.int32).at[exp_idx, slot_idx].set(row_idx, mode="drop")
    pick_gates = jnp.zeros((chosen.shape[1], per_expert), jnp.float32).at[exp_idx, slot_idx].set(gate_vals, mode="drop")
    return pick_rows, pick_gates


def expert_ffn(x_pack, w_gate, w_up, w_down, pick_gates):
    gate_act = jnp.einsum("lch,lhf->lcf", x_pack, w_gate, preferred_element_type=jnp.float32)
    up_act = jnp.einsum("lch,lhf->lcf", x_pack, w_up, preferred_element_type=jnp.float32)
    hidden_act = (jax.nn.silu(gate_act) * up_act).astype(jnp.bfloat16)
    expert_out = jnp.einsum("lcf,lfh->lch", hidden_act, w_down, preferred_element_type=jnp.float32)
    return expert_out * pick_gates[:, :, None]


def solution(mesh):
    ep_axes = tuple(mesh.axis_names)
    num_devices = math.prod(mesh.shape[axis_name] for axis_name in ep_axes)
    row_spec = P(ep_axes, None)
    w_spec = P(ep_axes, None, None)

    def local_layer(tokens, expert_ids, gate_weights, w_gate, w_up, w_down):
        tok_dev, hidden = tokens.shape
        top_k = expert_ids.shape[1]
        local_experts = w_gate.shape[0]
        capacity = tok_dev * top_k // num_devices
        rows_recv = num_devices * capacity
        per_expert = rows_recv // local_experts
        dest_dev = expert_ids // local_experts
        dev_hit = jnp.any(dest_dev[:, :, None] == jnp.arange(num_devices)[None, None, :], axis=1)
        all_experts = jnp.arange(num_devices * local_experts)
        gate_dense = jnp.sum(jnp.where(expert_ids[:, :, None] == all_experts[None, None, :], gate_weights[:, :, None], 0.0), axis=1)
        gate_dense = gate_dense.reshape(tok_dev, num_devices, local_experts)
        slot_pos = jnp.cumsum(dev_hit.astype(jnp.int32), axis=0) - 1
        place_mask = dev_hit[:, :, None] & (slot_pos[:, :, None] == jnp.arange(capacity)[None, None, :])
        place_bf = place_mask.astype(jnp.bfloat16)
        send_rows = jnp.einsum("tdc,th->dch", place_bf, tokens, preferred_element_type=jnp.float32).astype(jnp.bfloat16)
        send_gates = jnp.sum(jnp.where(place_mask[:, :, :, None], gate_dense[:, :, None, :], 0.0), axis=0)
        recv_rows = lax.all_to_all(send_rows, ep_axes, 0, 0, tiled=True)
        recv_gates = lax.all_to_all(send_gates, ep_axes, 0, 0, tiled=True)
        flat_rows = recv_rows.reshape(rows_recv, hidden)
        flat_gates = recv_gates.reshape(rows_recv, local_experts)
        pick_rows, pick_gates = pack_rows(flat_gates > 0.0, flat_gates, per_expert)
        weighted = expert_ffn(flat_rows[pick_rows], w_gate, w_up, w_down, pick_gates)
        part_sum = jax.ops.segment_sum(weighted.reshape(-1, hidden), pick_rows.reshape(-1), num_segments=rows_recv)
        back_rows = part_sum.astype(jnp.bfloat16).reshape(num_devices, capacity, hidden)
        returned = lax.all_to_all(back_rows, ep_axes, 0, 0, tiled=True)
        moe_sum = jnp.einsum("tdc,dch->th", place_bf, returned, preferred_element_type=jnp.float32)
        return (tokens.astype(jnp.float32) + moe_sum).astype(jnp.bfloat16)

    return jax.shard_map(local_layer, mesh=mesh, in_specs=(row_spec, row_spec, row_spec, w_spec, w_spec, w_spec), out_specs=row_spec, check_vma=False)
```

profile of v0, /device:TPU:0, one launch (start us, length us, event | category | flops | bytes accessed | tf_op | source)
XLA Modules:
  0.0 286.3 jit_solution(1983684396653799813)
XLA Ops:
  0.0 0.7 add_select_fusion
  0.7 0.6 reduce-window.14
  1.3 0.2 slice_reduce_fusion.1
  1.6 0.1 bitcast_bitcast_fusion.1
  1.6 0.8 select_reduce_fusion.1
  2.4 0.3 fusion.4
  2.7 1.8 select_reduce_fusion
  4.5 5.3 %all-to-all-start = ((f32[16,96,4]{1,2,0:T(4,128)}), f32[16,96,4]{1,2,0:T(4,128)S(1)}, u32[]{:S(2)}, u32[]{:S(2)}) async-start(f32[16,96,4]{1,2,0:T(4,128)} %select_reduce_fusion), calls=%async_computation | async-start | bytes 65536 | tf_op jit(solution)/shard_map/all_to_all | solution.py:50
  9.8 5.7 %convolution_convert_fusion = bf16[16,96,2048]{2,1,0:T(8,128)(2,1)} fusion(bf16[256,2048]{1,0:T(8,128)(2,1)} %param.6, s32[256,16]{0,1:T(8,128)S(1)} %bitcast_bitcast_fusion.1, pred[256,16]{0,1:T(8,128)(4,1)S(1)} %fusion.6), kind=kOutput, calls=%fused_computation.9 | convolution fusion | flops 1614544896 | bytes 7360512 | tf_op jit(solution)/shard_map/tdc,th->dch/dot_general | solution.py:47
  15.5 0.0 copy-start.2
  15.5 0.0 copy-start.1
  15.5 0.0 all-to-all-done
  15.6 3.9 %all-to-all-start.1 = ((bf16[16,96,2048]{2,1,0:T(8,128)(2,1)}), bf16[16,96,2048]{2,1,0:T(8,128)(2,1)}, u32[]{:S(2)}, u32[]{:S(2)}) async-start(bf16[16,96,2048]{2,1,0:T(8,128)(2,1)} %convolution_convert_fusion), calls=%async_computation.1 | async-start | bytes 12582912 | tf_op jit(solution)/shard_map/all_to_all | solution.py:49
  19.4 0.1 broadcast_in_dim.85
  19.5 0.4 reshape.96
  19.9 0.1 reshape.111
  20.1 1.2 reduce-window.16
  21.2 0.2 slice_reduce_fusion
  21.4 0.2 reduce-window.19
  21.6 0.3 copy.38
  21.9 0.4 reshape.102
  22.4 0.1 add_bitcast_fusion
  22.5 0.0 copy-done.2
  22.5 0.1 multiply_reduce_fusion
  22.6 0.0 copy-done.1
  22.6 0.1 and_reduce_fusion
  22.7 0.3 copy.37
  23.0 0.4 reshape.94
  23.4 23.0 %scatter_custom_fusion.2 = f32[1536]{0:T(1024)S(1)} fusion(s32[6144]{0:T(1024)S(1)} %reshape.94, f32[6144]{0:T(1024)S(1)} %reshape.102, f32[]{:T(128)} %constant.41.clone.1), kind=kCustom, calls=%fused_computation.46 | custom fusion | bytes 6148
  46.4 23.2 %scatter_custom_fusion.1 = s32[1536]{0:T(1024)S(1)} fusion(s32[6144]{0:T(1024)S(1)} %reshape.94, s32[6144]{0:T(1024)S(1)} %reshape.96, s32[]{:T(128)} %constant.20.clone.1), kind=kCustom, calls=%fused_computation.48 | custom fusion | bytes 6148 | tf_op jit(solution)/shard_map/broadcast_in_dim;reshape | solution.py:55
  69.7 30.2 %all-to-all-done.1 = bf16[16,96,2048]{2,1,0:T(8,128)(2,1)} async-done(((bf16[16,96,2048]{2,1,0:T(8,128)(2,1)}), bf16[16,96,2048]{2,1,0:T(8,128)(2,1)}, u32[]{:S(2)}, u32[]{:S(2)}) %all-to-all-start.1) | async-done | bytes 6291488 | tf_op jit(solution)/shard_map/all_to_all | solution.py:49
  99.9 16.3 %gather_fusion = bf16[1536,2048]{1,0:T(8,128)(2,1)} fusion(bf16[1536,2048]{1,0:T(8,128)(2,1)} %bitcast.6, s32[2048]{0:T(1024)S(1)} %pad_clamp_fusion), kind=kCustom, calls=%fused_computation | custom fusion | bytes 12589056 | tf_op jit(solution)/shard_map/gather | solution.py:54
  116.2 18.5 %fusion.17 = f32[4,384,1408]{2,1,0:T(8,128)} fusion(bf16[4,384,2048]{2,1,0:T(8,128)(2,1)} %bitcast.59, bf16[4,2048,1408]{2,1,0:T(8,128)(2,1)} %param.9), kind=kOutput, calls=%fused_computation.50 | convolution fusion | flops 8858370048 | bytes 38010880 | tf_op jit(solution)/shard_map/lch,lhf->lcf/dot_general | solution.py:19
  134.6 21.4 %multiply_convert_fusion = bf16[4,384,1408]{2,1,0:T(8,128)(2,1)} fusion(f32[4,384,1408]{2,1,0:T(8,128)} %fusion.17, bf16[4,384,2048]{2,1,0:T(8,128)(2,1)} %bitcast.60, bf16[4,2048,1408]{2,1,0:T(8,128)(2,1)} %param.10), kind=kOutput, calls=%fused_computation.4 | convolution fusion | flops 8871346176 | bytes 42336256 | tf_op jit(solution)/shard_map/lch,lhf->lcf/dot_general | solution.py:20
  156.0 18.4 %broadcast_multiply_fusion = f32[4,384,2048]{2,1,0:T(8,128)} fusion(f32[4,384]{1,0:T(4,128)S(1)} %reshape.74, bf16[4,384,1408]{2,1,0:T(8,128)(2,1)} %multiply_convert_fusion, bf16[4,1408,2048]{2,1,0:T(8,128)(2,1)} %param.11), kind=kOutput, calls=%fused_computation.5 | convolution fusion | flops 8861515776 | bytes 39983104 | tf_op jit(solution)/shard_map/lcf,lfh->lch/dot_general | solution.py:22
  174.4 26.1 %scatter_custom_fusion = f32[1536,2048]{1,0:T(8,128)} fusion(s32[1536]{0:T(1024)S(1)} %scatter_custom_fusion.1, f32[1536,2048]{1,0:T(8,128)} %bitcast.62, f32[]{:T(128)} %constant.41.clone.1), kind=kCustom, calls=%fused_computation.7 | custom fusion | flops 3145728 | bytes 12583424 | tf_op jit(solution)/shard_map/scatter-add | solution.py:55
  200.6 5.6 %convert_element_type.26 = bf16[1536,2048]{1,0:T(8,128)(2,1)S(1)} convert(f32[1536,2048]{1,0:T(8,128)} %scatter_custom_fusion) | non-fusion elementwise | flops 3145728 | bytes 18874368 | tf_op jit(solution)/shard_map/convert_element_type | solution.py:56
  206.1 0.0 copy-start
  206.1 77.3 %all_to_all.15 = bf16[16,96,2048]{2,1,0:T(8,128)(2,1)S(1)} all-to-all(bf16[16,96,2048]{2,1,0:T(8,128)(2,1)S(1)} %bitcast.58), channel_id=1, replica_groups=mesh['ez'=2,'ey'=2,'ex'=4] {'ez','ey','ex'}, dimensions={0} | all-to-all | bytes 12582912 | tf_op jit(solution)/shard_map/all_to_all | solution.py:57
  283.5 0.0 copy-done
  283.5 2.8 fusion.3
  (16 shorter events, 0.2 us)
Async XLA Ops:
  4.5 11.0 %all-to-all-start = ((f32[16,96,4]{1,2,0:T(4,128)}), f32[16,96,4]{1,2,0:T(4,128)S(1)}, u32[]{:S(2)}, u32[]{:S(2)}) async-start(f32[16,96,4]{1,2,0:T(4,128)} %select_reduce_fusion), calls=%async_computation | async-start | bytes 65536 | tf_op jit(solution)/shard_map/all_to_all | solution.py:50
  15.5 6.9 %copy-start.2 = (s32[2]{0:T(128)S(1)}, s32[2]{0:T(128)}, u32[]{:S(2)}) copy-start(s32[2]{0:T(128)} %constant.48) | copy-start | bytes 28
  15.5 7.0 %copy-start.1 = (s32[2]{0:T(128)S(1)}, s32[2]{0:T(128)}, u32[]{:S(2)}) copy-start(s32[2]{0:T(128)} %constant.51) | copy-start | bytes 28
  15.6 84.3 %all-to-all-start.1 = ((bf16[16,96,2048]{2,1,0:T(8,128)(2,1)}), bf16[16,96,2048]{2,1,0:T(8,128)(2,1)}, u32[]{:S(2)}, u32[]{:S(2)}) async-start(bf16[16,96,2048]{2,1,0:T(8,128)(2,1)} %convolution_convert_fusion), calls=%async_computation.1 | async-start | bytes 12582912 | tf_op jit(solution)/shard_map/all_to_all | solution.py:49
  206.1 77.4 %copy-start = (bf16[256,2048]{1,0:T(8,128)(2,1)S(1)}, bf16[256,2048]{1,0:T(8,128)(2,1)}, u32[]{:S(2)}) copy-start(bf16[256,2048]{1,0:T(8,128)(2,1)} %param.6) | copy-start | bytes 3145732
where the time goes:
time: 287 us; the launch traced here: 286 us
  blocking collectives  77.3 us (27%)
  matrix products  66.8 us (23%)
  local copies, waits for them, and re-layouts  64.9 us (23%)
  other arithmetic  37.7 us (13%)
  waiting for transfers between devices  30.2 us (11%)
  starting transfers between devices  9.16 us (3%)
    all_to_all x1, blocking collectives, local_layer(): returned = lax.all_to_all(back_rows, ep_axes, 0, 0, tiled=True)  77.3 us
    all_to_all x1, waiting for transfers between devices, local_layer(): recv_rows = lax.all_to_all(send_rows, ep_axes, 0, 0, tiled=True)  30.2 us
    scatter-add x1, other arithmetic, local_layer(): jax.ops.segment_sum(weighted.reshape(-1, hidden), pick_rows.reshape(-1),...  26.1 us
    unnamed x9, local copies, waits for them, and re-layouts  23.7 us
    another operation x1, local copies, waits for them, and re-layouts, local_layer(): jax.ops.segment_sum(weighted.reshape(-1, hidden), pick_rows.reshape(-1),...  23.2 us
    dot_general x1, matrix products, expert_ffn(): jnp.einsum('lch,lhf->lcf', x_pack, w_up, preferred_element_type=jnp.float32)  21.4 us
    dot_general x1, matrix products, expert_ffn(): jnp.einsum('lch,lhf->lcf', x_pack, w_gate, preferred_element_type=jnp.flo...  18.5 us
    dot_general x1, matrix products, expert_ffn(): jnp.einsum('lcf,lfh->lch', hidden_act, w_down, preferred_element_type=jnp...  18.4 us
  transfers between devices with their start and end apart: 2, of which 1 were waited for; matrix products, arithmetic and copies ran while one was open for 19% of the time, Pallas kernels for 0%

commit v1 on v0

v1 whole, which is shorter than its diff:
```python
import jax
import jax.numpy as jnp
from jax import lax
from jax.experimental import pallas as pl
from jax.experimental.pallas import tpu as pltpu
from jax.sharding import PartitionSpec as P

MESH = pl.DeviceIdType.MESH
BF, F32 = jnp.bfloat16, jnp.float32
TOK, HID, FF, NE, NDEV = 256, 2048, 1408, 4, 16
CAP = 96
PER = 384
SLOTS = NDEV * CAP
WIN = 128
CW = 256
NC = HID // CW
PARTS = ((0, 96), (96, 80), (176, 80))
FULL = slice(None)


def layer_kernel(x_hbm, w1_hbm, w3_hbm, w2_hbm, l1_ref, l2_ref, t_ref, gp_ref, st_ref, out_hbm,
                 x_all, acc_a, acc_b, h_act, slots, og, w13, w2b, xres, st0, st1, st2,
                 ag_send, ag_recv, rs_send, rs_recv, d_send, d_recv, w13_sem, w2_sem, loc_sem, credit):
    ez, ey, ex = lax.axis_index("ez"), lax.axis_index("ey"), lax.axis_index("ex")
    core = ex % 2
    pos = (ex // 2, ey, ez)

    def device(p, c):
        return (p[2], p[1], p[0] * 2 + c)

    def nbr(axis):
        p = list(pos)
        p[axis] = 1 - p[axis]
        return device(p, core)

    partner = device(pos, 1 - core)

    def cols(h):
        return pl.ds(pl.multiple_of(h * CW, CW), CW)

    def blocks(sel, c, rows, h):
        return x_all.at[sel[2], sel[1], sel[0], c, rows, cols(h)]

    def rows_of(k):
        return pl.ds(PARTS[k][0], PARTS[k][1])

    def pick(k, full, flip=()):
        sel = []
        for axis in range(3):
            if axis in full:
                sel.append(FULL)
            else:
                sel.append(1 - pos[axis] if axis in flip else pos[axis])
        return sel

    def ag(h, k, kind):
        a = [(k + i) % 3 for i in range(3)]
        if kind == 3:
            ref, to = blocks(pick(k, (a[0], a[1])), core, rows_of(k), h), partner
        elif kind == 4:
            ref, to = blocks(pick(k, (a[0], a[1]), (a[2],)), core, rows_of(k), h), partner
        else:
            ref, to = blocks(pick(k, tuple(a[:kind])), core, rows_of(k), h), nbr(a[kind])
        return pltpu.make_async_remote_copy(ref, ref, ag_send.at[h, k, kind], ag_recv.at[h, k, kind], device_id=to, device_id_type=MESH)

    def rs(h, k, kind):
        a = [(k + 2 - i) % 3 for i in range(3)]
        free = tuple(a[kind + 1:])
        src = blocks(pick(k, free, (a[kind],)), core, rows_of(k), h)
        if kind == 0:
            dst = st0.at[h % 2, :, :, rows_of(k), :]
        elif kind == 1:
            dst = st1.at[h % 2, :, rows_of(k), :]
        else:
            dst = st2.at[h % 2, rows_of(k), :]
        return pltpu.make_async_remote_copy(src, dst, rs_send.at[h, k, kind], rs_recv.at[h, k, kind], device_id=nbr(a[kind]), device_id_type=MESH)

    def cross(h):
        ref = blocks((FULL, FULL, FULL), 1 - core, FULL, h)
        return pltpu.make_async_remote_copy(ref, ref, d_send.at[h], d_recv.at[h], device_id=partner, device_id_type=MESH)

    def w13_copy(i, j):
        e, h = i % NE, i // NE
        src = (w1_hbm, w3_hbm)[j].at[e, pl.ds(pl.multiple_of(h * CW, CW), CW), :]
        return pltpu.make_async_copy(src, w13.at[i % 3, j], w13_sem.at[i % 3, j])

    def w2_copy(i):
        e, h = i % NE, i // NE
        return pltpu.make_async_copy(w2_hbm.at[e, :, cols(h)], w2b.at[i % 3], w2_sem.at[i % 3])

    own = pltpu.make_async_copy(x_hbm, x_all.at[pos[2], pos[1], pos[0], core], loc_sem.at[0])
    own.start()
    res = pltpu.make_async_copy(x_hbm, xres, loc_sem.at[1])
    res.start()
    for i in range(2):
        for j in range(2):
            w13_copy(i, j).start()

    barrier = pltpu.get_barrier_semaphore()
    for to in (nbr(0), nbr(1), nbr(2), partner):
        pl.semaphore_signal(barrier, inc=1, device_id=to, device_id_type=MESH)
    own.wait()
    pl.semaphore_wait(barrier, 4)

    def start(h, kind):
        for k in range(3):
            ag(h, k, kind).start()

    def arrive(h, kind):
        for k in range(3):
            ag(h, k, kind).wait_recv()

    for h in range(4):
        start(h, 0)

    def zero(i, _):
        acc_a[pl.ds(i * 128, 128), :] = jnp.zeros((128, FF), F32)
        acc_b[pl.ds(i * 128, 128), :] = jnp.zeros((128, FF), F32)
        return 0
    lax.fori_loop(0, NE * PER // 128, zero, 0)

    for h in range(2):
        arrive(h, 0)
        start(h, 1)

    def compact(h):
        def body(s, _):
            blk = x_all[s // 8, (s // 4) % 2, (s // 2) % 2, s % 2, :, cols(h)]
            slots[pl.ds(pl.multiple_of(s * CAP, CAP), CAP), :] = jnp.dot(l1_ref[s], blk, preferred_element_type=F32).astype(BF)
            return 0
        lax.fori_loop(0, NDEV, body, 0)

    def expert_in(h, e):
        i = h * NE + e
        for j in range(2):
            w13_copy(i, j).wait()

        @pl.when(i + 2 < NC * NE)
        def _():
            for j in range(2):
                w13_copy(i + 2, j).start()
        rows = pl.ds(pl.multiple_of(e * PER, PER), PER)
        xe = jnp.dot(l2_ref[rows, :], slots[...], preferred_element_type=F32).astype(BF)
        acc_a[rows, :] += jnp.dot(xe, w13[i % 3, 0], preferred_element_type=F32)
        acc_b[rows, :] += jnp.dot(xe, w13[i % 3, 1], preferred_element_type=F32)

    def experts_in(h, lo, hi):
        def body(e, _):
            expert_in(h, e)
            return 0
        lax.fori_loop(lo, hi, body, 0)

    def step_in(h, _):
        @pl.when(h < NC)
        def _():
            arrive(h, 1)
            start(h, 2)
            start(h, 3)

        @pl.when(h >= 1)
        def _():
            arrive(h - 1, 3)
            arrive(h - 1, 4)
            compact(h - 1)
            experts_in(h - 1, 0, 1)

        @pl.when(h + 2 < NC)
        def _():
            arrive(h + 2, 0)
            start(h + 2, 1)

        @pl.when(h + 4 < NC)
        def _():
            start(h + 4, 0)

        @pl.when(h >= 1)
        def _():
            experts_in(h - 1, 1, NE)

        @pl.when(h < NC)
        def _():
            arrive(h, 2)
            start(h, 4)
        return 0

    lax.fori_loop(0, NC + 1, step_in, 0)

    def drain(h, _):
        for k in range(3):
            for kind in range(5):
                ag(h, k, kind).wait_send()
        return 0
    lax.fori_loop(0, NC, drain, 0)
    pl.semaphore_signal(credit, inc=1, device_id=partner, device_id_type=MESH)
    for i in range(2):
        w2_copy(i).start()

    def activate(i, _):
        rows = pl.ds(pl.multiple_of(i * 32, 32), 32)
        a = acc_a[rows, :]
        h_act[rows, :] = (a * jax.nn.sigmoid(a) * acc_b[rows, :]).astype(BF)
        return 0
    lax.fori_loop(0, NE * PER // 32, activate, 0)
    res.wait()

    def expert_out(h):
        def body(e, _):
            i = h * NE + e
            w2_copy(i).wait()

            @pl.when(i + 2 < NC * NE)
            def _():
                w2_copy(i + 2).start()
            rows = pl.ds(pl.multiple_of(e * PER, PER), PER)
            o = jnp.dot(h_act[rows, :], w2b[i % 3], preferred_element_type=F32) * gp_ref[rows, :]
            high = o.astype(BF)
            tiles = pl.ds(e * (PER // 16), PER // 16)
            og[0, tiles] = high.reshape(PER // 16, 16, CW)
            og[1, tiles] = (o - high.astype(F32)).astype(BF).reshape(PER // 16, 16, CW)
            return 0
        lax.fori_loop(0, NE, body, 0)

    def spread(s):
        total = None
        for half in range(2):
            rhs = jnp.concatenate([og[half, pl.ds(st_ref[s * NE + e], WIN // 16)].reshape(WIN, CW) for e in range(NE)], axis=0)
            part = jnp.dot(t_ref[s], rhs, preferred_element_type=F32)
            total = part if total is None else total + part
        return total

    def spread_other(h):
        def body(j, _):
            x_all[j // 4, (j // 2) % 2, j % 2, 1 - core, :, cols(h)] = spread(j * 2 + 1 - core).astype(BF)
            return 0
        lax.fori_loop(0, NDEV // 2, body, 0)

    def spread_mine(h):
        def body(j, _):
            idx = (j // 4, (j // 2) % 2, j % 2, core, FULL, cols(h))
            x_all[idx] = (spread(j * 2 + core) + x_all[idx].astype(F32)).astype(BF)
            return 0
        lax.fori_loop(0, NDEV // 2, body, 0)

    def add_in(h, kind):
        for k in range(3):
            rs(h, k, kind).wait_recv()
            a = [(k + 2 - i) % 3 for i in range(3)]
            free = a[kind + 1:]
            rows = rows_of(k)
            if kind == 2:
                sel = pos
                mine = x_all[sel[2], sel[1], sel[0], core, rows, cols(h)].astype(F32) + st2[h % 2, rows, :].astype(F32)
                xres[rows, cols(h)] = (xres[rows, cols(h)].astype(F32) + mine).astype(BF)
                continue
            order = sorted(free, reverse=True)
            for n in range(2 ** len(order)):
                sel = list(pos)
                bits = [(n >> (len(order) - 1 - b)) & 1 for b in range(len(order))]
                for axis, bit in zip(order, bits):
                    sel[axis] = bit
                got = st0[h % 2, bits[0], bits[1], rows, :] if kind == 0 else st1[h % 2, bits[0], rows, :]
                idx = (sel[2], sel[1], sel[0], core, rows, cols(h))
                x_all[idx] = (x_all[idx].astype(F32) + got.astype(F32)).astype(BF)

    def step_out(h, _):
        @pl.when(h < NC)
        def _():
            expert_out(h)
            spread_other(h)

            @pl.when(h == 0)
            def _():
                pl.semaphore_wait(credit, 1)
            cross(h).start()

        @pl.when(jnp.logical_and(h >= 1, h < NC + 1))
        def _():
            add_in(h - 1, 0)
            for k in range(3):
                rs(h - 1, k, 1).start()

        @pl.when(h < NC)
        def _():
            cross(h).wait_recv()
            spread_mine(h)
            for k in range(3):
                rs(h, k, 0).start()

        @pl.when(jnp.logical_and(h >= 1, h < NC + 1))
        def _():
            add_in(h - 1, 1)
            for k in range(3):
                rs(h - 1, k, 2).start()

        @pl.when(h >= 2)
        def _():
            add_in(h - 2, 2)
        return 0

    lax.fori_loop(0, NC + 2, step_out, 0)

    def drain_out(h, _):
        for k in range(3):
            for kind in range(3):
                rs(h, k, kind).wait_send()
        cross(h).wait_send()
        return 0
    lax.fori_loop(0, NC, drain_out, 0)
    fin = pltpu.make_async_copy(xres, out_hbm, loc_sem.at[0])
    fin.start()
    fin.wait()


def route(ids, gates, ep_axes):
    dense_g = []
    for_all = jnp.arange(NDEV * NE)
    match = ids[:, :, None] == for_all[None, None, :]
    dense_g = jnp.sum(jnp.where(match, gates[:, :, None], 0.0), axis=1)
    dense_m = jnp.any(match, axis=1).astype(F32)
    both = jnp.stack([dense_g.T.reshape(NDEV, NE, TOK), dense_m.T.reshape(NDEV, NE, TOK)], axis=1)
    got = lax.all_to_all(both, ep_axes, 0, 0, tiled=True)
    gate, has = got[:, 0], got[:, 1] > 0.5
    hit = jnp.any(has, axis=1)
    slot = jnp.cumsum(hit.astype(jnp.int32), axis=1) - 1
    l1 = (hit[:, None, :] & (slot[:, None, :] == jnp.arange(CAP)[None, :, None]))
    within = jnp.cumsum(has.astype(jnp.int32), axis=2)
    count = within[:, :, -1]
    base = jnp.cumsum(count, axis=0) - count
    rank = base[:, :, None] + within - 1
    begin = jnp.minimum(base // 16 * 16, PER - WIN)
    l1f = l1.astype(F32)
    pick = lambda v: jnp.sum(jnp.where(l1[:, None, :, :], v[:, :, None, :], 0), axis=-1)
    slot_rank = pick(jnp.where(has, rank + 1, 0)) - 1
    l2 = slot_rank.transpose(1, 0, 2).reshape(NE, 1, SLOTS) == jnp.arange(PER)[None, :, None]
    slot_gate = pick(gate).transpose(1, 0, 2).reshape(NE, 1, SLOTS)
    gp = jnp.sum(jnp.where(l2, slot_gate, 0.0), axis=2).reshape(NE * PER, 1)
    at = jnp.where(has, rank - begin[:, :, None], -1).transpose(0, 2, 1)
    t = (at[:, :, :, None] == jnp.arange(WIN)[None, None, None, :]).reshape(NDEV, TOK, NE * WIN)
    return l1.astype(BF), l2.reshape(NE * PER, SLOTS).astype(BF), t.astype(BF), gp, (begin // 16 + jnp.arange(NE)[None, :] * (PER // 16)).reshape(-1).astype(jnp.int32)


def solution(mesh):
    ep_axes = tuple(mesh.axis_names)
    row_spec, w_spec = P(ep_axes, None), P(ep_axes, None, None)
    vmem, anyspace = pl.BlockSpec(memory_space=pltpu.VMEM), pl.BlockSpec(memory_space=pl.ANY)

    def local_layer(tokens, ids, gates, w1, w3, w2):
        l1, l2, t, gp, begin = route(ids, gates, ep_axes)
        return pl.pallas_call(
            layer_kernel,
            name="moe_layer",
            out_shape=jax.ShapeDtypeStruct((TOK, HID), BF),
            in_specs=[anyspace] * 4 + [vmem] * 4 + [pl.BlockSpec(memory_space=pltpu.SMEM)],
            out_specs=anyspace,
            scratch_shapes=[
                pltpu.VMEM((2, 2, 2, 2, TOK, HID), BF),
                pltpu.VMEM((NE * PER, FF), F32),
                pltpu.VMEM((NE * PER, FF), F32),
                pltpu.VMEM((NE * PER, FF), BF),
                pltpu.VMEM((SLOTS, CW), BF),
                pltpu.VMEM((2, NE * PER // 16, 16, CW), BF),
                pltpu.VMEM((3, 2, CW, FF), BF),
                pltpu.VMEM((3, FF, CW), BF),
                pltpu.VMEM((TOK, HID), BF),
                pltpu.VMEM((2, 2, 2, TOK, CW), BF),
                pltpu.VMEM((2, 2, TOK, CW), BF),
                pltpu.VMEM((2, TOK, CW), BF),
                pltpu.SemaphoreType.DMA((NC, 3, 5)),
                pltpu.SemaphoreType.DMA((NC, 3, 5)),
                pltpu.SemaphoreType.DMA((NC, 3, 3)),
                pltpu.SemaphoreType.DMA((NC, 3, 3)),
                pltpu.SemaphoreType.DMA((NC,)),
                pltpu.SemaphoreType.DMA((NC,)),
                pltpu.SemaphoreType.DMA((3, 2)),
                pltpu.SemaphoreType.DMA((3,)),
                pltpu.SemaphoreType.DMA((2,)),
                pltpu.SemaphoreType.REGULAR,
            ],
            compiler_params=pltpu.CompilerParams(collective_id=0, has_side_effects=True, vmem_limit_bytes=67_043_328),
        )(tokens, w1, w3, w2, l1, l2, t, gp, begin)

    return jax.shard_map(local_layer, mesh=mesh, in_specs=(row_spec, row_spec, row_spec, w_spec, w_spec, w_spec), out_specs=row_spec, check_vma=False)
```

time: 287 us -> 265 us (0.923)
  Pallas kernels: 0 us -> 209 us
  blocking collectives: 77.3 us -> 0 us
  matrix products: 66.8 us -> 0 us
  local copies, waits for them, and re-layouts: 64.9 us -> 23 us
  waiting for transfers between devices: 30.2 us -> 5.95 us
  other arithmetic: 37.7 us -> 20.3 us
  starting transfers between devices: 9.16 us -> 5.29 us
    pallas_call x0 -> x1, Pallas kernels: none -> 209 us  [local_layer(): pl.pallas_call(layer_kernel, name='moe_layer', out_shape=jax.ShapeDtypeSt...]
    all_to_all x1 -> x0, blocking collectives: 77.3 us -> none  [local_layer(): returned = lax.all_to_all(back_rows, ep_axes, 0, 0, tiled=True)]
    dot_general x5 -> x0, matrix products: 66.8 us -> none  [the longest x1 21.4 us: expert_ffn(): jnp.einsum('lch,lhf->lcf', x_pack, w_up, preferred_element_type=jnp.float32)]
    scatter-add x1 -> x0, other arithmetic: 26.1 us -> none  [local_layer(): jax.ops.segment_sum(weighted.reshape(-1, hidden), pick_rows.reshape(-1),...]
    all_to_all x2 -> x1, waiting for transfers between devices: 30.2 us -> 5.95 us  [route(): got = lax.all_to_all(both, ep_axes, 0, 0, tiled=True)]
    another operation x4 -> x8, local copies, waits for them, and re-layouts: 23.4 us -> 1.32 us  [the longest x3 0.71 us: route(): jnp.stack([dense_g.T.reshape(NDEV, NE, TOK), dense_m.T.reshape(NDEV, NE,...]
    unnamed x9 -> x3, local copies, waits for them, and re-layouts: 23.7 us -> 3.52 us
    eq x0 -> x6, local copies, waits for them, and re-layouts: none -> 16.7 us  [the longest x3 16.6 us: route(): at[:, :, :, None] == jnp.arange(WIN)[None, None, None, :]]
  transfers between devices with their start and end apart: 2 -> 1, of which waited for: 1 -> 1; matrix products, arithmetic and copies ran while one was open for 19% -> 0% of each run, Pallas kernels for 0% -> 0%
where the time goes in v1:
time: 265 us; the launch traced here: 264 us
  Pallas kernels  209 us (79%)
  local copies, waits for them, and re-layouts  23 us (9%)
  other arithmetic  20.3 us (8%)
  waiting for transfers between devices  5.95 us (2%)
  starting transfers between devices  5.29 us (2%)
    pallas_call x1, Pallas kernels, local_layer(): pl.pallas_call(layer_kernel, name='moe_layer', out_shape=jax.ShapeDtypeSt...  209 us
    eq x3, local copies, waits for them, and re-layouts, route(): at[:, :, :, None] == jnp.arange(WIN)[None, None, None, :]  16.6 us
    convert_element_type x1, other arithmetic, route(): t.astype(BF)  6.59 us
    all_to_all x1, waiting for transfers between devices, route(): got = lax.all_to_all(both, ep_axes, 0, 0, tiled=True)  5.95 us
  transfers between devices with their start and end apart: 1, of which 1 were waited for; matrix products, arithmetic and copies ran while one was open for 0% of the time, Pallas kernels for 0%

profile of v1, /device:TPU:0, one launch (start us, length us, event | category | flops | bytes accessed | tf_op | source)
XLA Modules:
  0.0 264.0 jit_solution(1981580453479495291)
XLA Ops:
  0.0 0.7 fusion.2
  0.8 0.8 select_reduce_fusion.3
  1.6 0.7 copy.74
  2.3 5.3 %all-to-all-start = ((f32[16,2,4,256]{3,2,1,0:T(4,128)}), f32[16,2,4,256]{3,2,1,0:T(4,128)S(1)}, u32[]{:S(2)}, u32[]{:S(2)}) async-start(f32[16,2,4,256]{3,2,1,0:T(4,128)} %copy.74), calls=%async_computation | async-start | bytes 262144 | tf_op jit(solution)/shard_map/all_to_all | solution.py:321
  7.6 0.1 add.55
  7.7 6.0 %all-to-all-done = f32[16,2,4,256]{3,2,1,0:T(4,128)S(1)} async-done(((f32[16,2,4,256]{3,2,1,0:T(4,128)}), f32[16,2,4,256]{3,2,1,0:T(4,128)S(1)}, u32[]{:S(2)}, u32[]{:S(2)}) %all-to-all-start) | async-done | bytes 131104 | tf_op jit(solution)/shard_map/all_to_all | solution.py:321
  13.8 0.6 reduce-window.14
  14.4 0.2 slice_reduce_fusion.1
  14.6 0.1 copy_bitcast_fusion.1
  14.7 1.3 fusion.1
  16.0 2.3 reduce-window.16
  18.3 0.3 slice_reduce_fusion
  18.6 0.1 copy_bitcast_fusion
  18.7 0.1 slice.32
  18.8 0.2 copy.89
  19.0 0.1 squeeze.7
  19.1 0.1 reduce_window_sum.56
  19.2 0.2 copy.82
  19.4 0.3 fusion.6
  19.7 0.1 select_bitcast_fusion
  19.9 1.2 select_reduce_fusion.2
  21.1 0.1 eq.82
  21.2 0.6 copy.85
  21.9 6.3 %eq.89 = s32[16,256,4,128]{3,2,1,0:T(4,128)} broadcast(s32[16,256,4]{2,1,0:T(8,128)S(1)} %copy.85), dimensions={0,1,2} | broadcast | bytes 8454144 | tf_op jit(solution)/shard_map/eq | solution.py:338
  28.2 10.3 %eq.90 = s32[16,256,512]{2,1,0:T(8,128)} reshape(s32[16,256,4,128]{3,2,1,0:T(4,128)} %eq.89) | data formatting | bytes 16777216 | tf_op jit(solution)/shard_map/eq | solution.py:338
  38.5 1.2 select_reduce_fusion.1
  39.7 0.1 broadcast_in_dim.92
  39.8 3.0 %fusion.l2_ref = bf16[1536,1536]{1,0:T(8,128)(2,1)} fusion(s32[1536]{0:T(1024)S(1)} %eq.86, s32[4,1536]{1,0:T(4,128)S(1)} %eq.82), kind=kLoop, calls=%fused_computation.3 | loop fusion | flops 4718592 | bytes 4749312 | tf_op jit(solution)/shard_map/convert_element_type | solution.py:339
  42.8 1.2 select_reduce_fusion
  44.0 1.2 copy.97
  45.2 6.6 %compare_convert_fusion.t_ref = bf16[16,256,512]{2,1,0:T(8,128)(2,1)} fusion(s32[16,256,512]{2,1,0:T(8,128)} %eq.90, s32[512]{0:T(512)S(1)} %iota_bitcast_fusion), kind=kLoop, calls=%fused_computation.4 | loop fusion | flops 4194304 | bytes 12584960 | tf_op jit(solution)/shard_map/convert_element_type | solution.py:339
  51.8 0.6 fusion.8.st_ref
  52.4 209.3 %moe_layer.1 = bf16[256,2048]{1,0:T(8,128)(2,1)} custom-call(bf16[256,2048]{1,0:T(8,128)(2,1)} %x_hbm.1, bf16[4,2048,1408]{2,1,0:T(8,128)(2,1)} %w1_hbm.1, bf16[4,2048,1408]{2,1,0:T(8,128)(2,1)} %w3_hbm.1, bf16[4,1408,2048]{2,1,0:T(8,128)(2,1)} %w2_hbm.1, bf16[16,96,256]{2,1,0:T(8,128)(2,1)} %get-tuple-element.14.l1_ref, bf16[1536,1536]{1,0:T(8,128)(2,1)} %fusion.l2_ref, ...), custom_call_target="tpu_custom_call" | custom-call | tf_op jit(solution)/shard_map/moe_layer/pallas_call | solution.py:349
  261.7 2.3 copy.108
  (25 shorter events, 0.4 us)
Async XLA Ops:
  2.3 11.4 %all-to-all-start = ((f32[16,2,4,256]{3,2,1,0:T(4,128)}), f32[16,2,4,256]{3,2,1,0:T(4,128)S(1)}, u32[]{:S(2)}, u32[]{:S(2)}) async-start(f32[16,2,4,256]{3,2,1,0:T(4,128)} %copy.74), calls=%async_computation | async-start | bytes 262144 | tf_op jit(solution)/shard_map/all_to_all | solution.py:321

commit v2 on v1

--- a/solution.py
+++ b/solution.py
@@ -18,9 +18,12 @@
 FULL = slice(None)
 
 
-def layer_kernel(x_hbm, w1_hbm, w3_hbm, w2_hbm, l1_ref, l2_ref, t_ref, gp_ref, st_ref, out_hbm,
-                 x_all, acc_a, acc_b, h_act, slots, og, w13, w2b, xres, st0, st1, st2,
-                 ag_send, ag_recv, rs_send, rs_recv, d_send, d_recv, w13_sem, w2_sem, loc_sem, credit):
+def layer_kernel(x_hbm, meta_ref, w1_hbm, w3_hbm, w2_hbm, out_hbm,
+                 x_all, acc_a, acc_b, h_act, og, w13, w2b, xres, st0, st1, st2,
+                 l1_ref, l2_ref, t_ref, gp_ref, meta, mrow, crow, at_rows, split, rslot, colq, st_ref,
+                 ag_send, ag_recv, rs_send, rs_recv, d_send, d_recv, w13_sem, w2_sem, loc_sem, m_send, m_recv, credit):
+    slots = h_act.at[:, 2 * CW:3 * CW]
+    sgate = h_act.at[:, 3 * CW:3 * CW + 128]
     ez, ey, ex = lax.axis_index("ez"), lax.axis_index("ey"), lax.axis_index("ex")
     core = ex % 2
     pos = (ex // 2, ey, ez)
@@ -80,27 +83,41 @@
         return pltpu.make_async_remote_copy(ref, ref, d_send.at[h], d_recv.at[h], device_id=partner, device_id_type=MESH)
 
     def w13_copy(i, j):
-        e, h = i % NE, i // NE
-        src = (w1_hbm, w3_hbm)[j].at[e, pl.ds(pl.multiple_of(h * CW, CW), CW), :]
-        return pltpu.make_async_copy(src, w13.at[i % 3, j], w13_sem.at[i % 3, j])
+        e, g = i % NE, i // NE
+        src = (w1_hbm, w3_hbm)[j].at[e, pl.ds(pl.multiple_of(g * 2 * CW, 2 * CW), 2 * CW), :]
+        return pltpu.make_async_copy(src, w13.at[i % 2, j], w13_sem.at[i % 2, j])
 
     def w2_copy(i):
         e, h = i % NE, i // NE
-        return pltpu.make_async_copy(w2_hbm.at[e, :, cols(h)], w2b.at[i % 3], w2_sem.at[i % 3])
+        return pltpu.make_async_copy(w2_hbm.at[e, :, cols(h)], w2b.at[i % 4], w2_sem.at[i % 4])
+
+    me = ez * 8 + ey * 4 + ex
+
+    def meta_copy(i):
+        to = (me + i) % NDEV
+        return pltpu.make_async_remote_copy(meta_ref.at[to], meta.at[me], m_send.at[i], m_recv.at[i],
+                                            device_id=(to // 8, (to // 4) % 2, to % 4), device_id_type=MESH)
+
+    def meta_from(i):
+        src = (me + NDEV - i) % NDEV
+        return pltpu.make_async_remote_copy(meta_ref.at[0], meta.at[src], m_send.at[i], m_recv.at[i],
+                                            device_id=(0, 0, 0), device_id_type=MESH)
 
     own = pltpu.make_async_copy(x_hbm, x_all.at[pos[2], pos[1], pos[0], core], loc_sem.at[0])
     own.start()
     res = pltpu.make_async_copy(x_hbm, xres, loc_sem.at[1])
     res.start()
-    for i in range(2):
-        for j in range(2):
-            w13_copy(i, j).start()
+    for j in range(2):
+        w13_copy(0, j).start()
 
     barrier = pltpu.get_barrier_semaphore()
-    for to in (nbr(0), nbr(1), nbr(2), partner):
-        pl.semaphore_signal(barrier, inc=1, device_id=to, device_id_type=MESH)
+    for i in range(1, NDEV):
+        to = (me + i) % NDEV
+        pl.semaphore_signal(barrier, inc=1, device_id=(to // 8, (to // 4) % 2, to % 4), device_id_type=MESH)
     own.wait()
-    pl.semaphore_wait(barrier, 4)
+    pl.semaphore_wait(barrier, NDEV - 1)
+    for i in range(1, NDEV):
+        meta_copy(i).start()
 
     def start(h, kind):
         for k in range(3):
@@ -123,32 +140,106 @@
         arrive(h, 0)
         start(h, 1)
 
+    meta[me] = meta_ref[me]
+    for i in range(1, NDEV):
+        meta_from(i).wait_recv()
+
+    def times_t(lhs, rhs):
+        return lax.dot_general(lhs, rhs, (((1,), (1,)), ((), ())), preferred_element_type=F32)
+
+    for s in range(NDEV):
+        g = meta[s]
+        m = jnp.where(g > 0.0, 1.0, 0.0)
+        mrow[s * 8:s * 8 + 8, :] = jnp.concatenate([m, jnp.max(m, axis=0, keepdims=True), jnp.zeros((3, TOK), F32)], axis=0)
+        g1 = g.astype(BF).astype(F32)
+        g2 = (g - g1).astype(BF).astype(F32)
+        g3 = g - g1 - g2
+        split[s] = jnp.concatenate([g1, g2, g3, jnp.zeros((4, TOK), F32)], axis=0).astype(BF)
+    c = mrow[...]
+    lane = lax.broadcasted_iota(jnp.int32, c.shape, 1)
+    for n in range(8):
+        c = c + jnp.where(lane >= 2 ** n, pltpu.roll(c, 2 ** n, 1), 0.0)
+    crow[...] = c
+
+    base = jnp.zeros((8, 1), F32)
+    pieces = []
+    for s in range(NDEV):
+        m, c = mrow[s * 8:s * 8 + 8, :], crow[s * 8:s * 8 + 8, :]
+        has = m > 0.5
+        begin = jnp.minimum(jnp.floor(base * (1 / 16)) * 16, float(PER - WIN))
+        at_rows[s * 8:s * 8 + 8, :] = jnp.where(has, base + c - begin, 0.0)
+        rank = jnp.where(has, base + c, 0.0)
+        high = jnp.floor(rank * (1 / 128))
+        spot = lax.broadcasted_iota(jnp.int32, (CAP, TOK), 0).astype(F32)
+        l1 = jnp.where(jnp.where(has, c, 0.0)[4:5, :] == spot + 1.0, 1.0, 0.0).astype(BF)
+        l1_ref[s] = l1
+        both = jnp.concatenate([rank - 128 * high, high], axis=0).astype(BF)
+        got = times_t(both, l1)
+        pieces.append(got[0:8, :] + 128 * got[8:16, :])
+        if s % 4 == 3:
+            rslot[:, (s // 4) * 4 * CAP:(s // 4 + 1) * 4 * CAP] = jnp.concatenate(pieces, axis=1)
+            pieces = []
+        for e in range(NE):
+            st_ref[s * NE + e] = jnp.clip(jnp.sum(begin[e:e + 1, :]).astype(jnp.int32) // 16, 0, (PER - WIN) // 16) + e * (PER // 16)
+        base = base + c[:, TOK - 1:TOK]
+    eye = (lax.broadcasted_iota(jnp.int32, (TOK, TOK), 0) == lax.broadcasted_iota(jnp.int32, (TOK, TOK), 1))
+    colq[...] = times_t(jnp.where(eye, 1.0, 0.0).astype(BF), at_rows[...].astype(BF))
+
+    def fill_l2(b, _):
+        for e in range(NE):
+            p = lax.broadcasted_iota(jnp.int32, (32, SLOTS), 0) + (b * 32 + 1)
+            l2_ref[pl.ds(pl.multiple_of(e * PER + b * 32, 32), 32), :] = jnp.where(rslot[e:e + 1, :] == p.astype(F32), 1.0, 0.0).astype(BF)
+        return 0
+    lax.fori_loop(0, PER // 32, fill_l2, 0)
+
+    def gate_rows():
+        for s in range(NDEV):
+            got = times_t(l1_ref[s], split[s])
+            sgate[s * CAP:(s + 1) * CAP, :] = jnp.concatenate([got, jnp.zeros((CAP, 112), F32)], axis=1).astype(BF)
+
+        for e in range(NE):
+            rows = slice(e * PER, (e + 1) * PER)
+            got = jnp.dot(l2_ref[rows, :], sgate[...], preferred_element_type=F32)
+            gp_ref[rows, :] = got[:, e:e + 1] + got[:, NE + e:NE + e + 1] + got[:, 2 * NE + e:2 * NE + e + 1]
+
+    def fill_t(s):
+        q = pltpu.roll(colq[...], 128 - s * 8, 1)
+        place = lax.broadcasted_iota(jnp.int32, (TOK, WIN), 1).astype(F32) + 1.0
+        t_ref[s] = jnp.concatenate([jnp.where(q[:, e:e + 1] == place, 1.0, 0.0).astype(BF) for e in range(NE)], axis=1)
+
     def compact(h):
-        def body(s, _):
+        for s in range(NDEV):
             blk = x_all[s // 8, (s // 4) % 2, (s // 2) % 2, s % 2, :, cols(h)]
-            slots[pl.ds(pl.multiple_of(s * CAP, CAP), CAP), :] = jnp.dot(l1_ref[s], blk, preferred_element_type=F32).astype(BF)
+            slots[s * CAP:(s + 1) * CAP, :] = jnp.dot(l1_ref[s], blk, preferred_element_type=F32).astype(BF)
+
+    def pack(h):
+        def body(n, _):
+            for e in range(2):
+                rows = pl.ds(pl.multiple_of((2 * n + e) * PER, PER), PER)
+                h_act[rows, pl.ds(pl.multiple_of((h % 2) * CW, CW), CW)] = jnp.dot(l2_ref[rows, :], slots[...], preferred_element_type=F32).astype(BF)
             return 0
-        lax.fori_loop(0, NDEV, body, 0)
-
-    def expert_in(h, e):
-        i = h * NE + e
+        lax.fori_loop(0, NE // 2, body, 0)
+
+    def expert_in(g, e):
+        i = g * NE + e
         for j in range(2):
             w13_copy(i, j).wait()
 
-        @pl.when(i + 2 < NC * NE)
+        @pl.when(i + 1 < NC // 2 * NE)
         def _():
             for j in range(2):
-                w13_copy(i + 2, j).start()
+                w13_copy(i + 1, j).start()
+
         rows = pl.ds(pl.multiple_of(e * PER, PER), PER)
-        xe = jnp.dot(l2_ref[rows, :], slots[...], preferred_element_type=F32).astype(BF)
-        acc_a[rows, :] += jnp.dot(xe, w13[i % 3, 0], preferred_element_type=F32)
-        acc_b[rows, :] += jnp.dot(xe, w13[i % 3, 1], preferred_element_type=F32)
-
-    def experts_in(h, lo, hi):
+        xe = h_act[rows, :2 * CW]
+        acc_a[rows, :] += jnp.dot(xe, w13[i % 2, 0], preferred_element_type=F32)
+        acc_b[rows, :] += jnp.dot(xe, w13[i % 2, 1], preferred_element_type=F32)
+
+    def experts_in(g):
         def body(e, _):
-            expert_in(h, e)
+            expert_in(g, e)
             return 0
-        lax.fori_loop(lo, hi, body, 0)
+        lax.fori_loop(0, NE, body, 0)
 
     def step_in(h, _):
         @pl.when(h < NC)
@@ -162,7 +253,7 @@
             arrive(h - 1, 3)
             arrive(h - 1, 4)
             compact(h - 1)
-            experts_in(h - 1, 0, 1)
+            pack(h - 1)
 
         @pl.when(h + 2 < NC)
         def _():
@@ -173,9 +264,14 @@
         def _():
             start(h + 4, 0)
 
-        @pl.when(h >= 1)
-        def _():
-            experts_in(h - 1, 1, NE)
+        @pl.when(jnp.logical_and(h >= 1, h % 2 == 0))
+        def _():
+            experts_in((h - 1) // 2)
+
+        @pl.when(h < NC)
+        def _():
+            fill_t(2 * h)
+            fill_t(2 * h + 1)
 
         @pl.when(h < NC)
         def _():
@@ -184,6 +280,7 @@
         return 0
 
     lax.fori_loop(0, NC + 1, step_in, 0)
+    gate_rows()
 
     def drain(h, _):
         for k in range(3):
@@ -191,6 +288,8 @@
                 ag(h, k, kind).wait_send()
         return 0
     lax.fori_loop(0, NC, drain, 0)
+    for i in range(1, NDEV):
+        meta_copy(i).wait_send()
     pl.semaphore_signal(credit, inc=1, device_id=partner, device_id_type=MESH)
     for i in range(2):
         w2_copy(i).start()
@@ -204,21 +303,24 @@
     res.wait()
 
     def expert_out(h):
-        def body(e, _):
-            i = h * NE + e
+        def body(n, _):
+            i = h * NE + 2 * n
             w2_copy(i).wait()
+            w2_copy(i + 1).wait()
 
             @pl.when(i + 2 < NC * NE)
             def _():
                 w2_copy(i + 2).start()
-            rows = pl.ds(pl.multiple_of(e * PER, PER), PER)
-            o = jnp.dot(h_act[rows, :], w2b[i % 3], preferred_element_type=F32) * gp_ref[rows, :]
-            high = o.astype(BF)
-            tiles = pl.ds(e * (PER // 16), PER // 16)
-            og[0, tiles] = high.reshape(PER // 16, 16, CW)
-            og[1, tiles] = (o - high.astype(F32)).astype(BF).reshape(PER // 16, 16, CW)
+                w2_copy(i + 3).start()
+            for e in range(2):
+                rows = pl.ds(pl.multiple_of((2 * n + e) * PER, PER), PER)
+                o = jnp.dot(h_act[rows, :], w2b[(i + e) % 4], preferred_element_type=F32) * gp_ref[rows, :]
+                high = o.astype(BF)
+                tiles = pl.ds((2 * n + e) * (PER // 16), PER // 16)
+                og[0, tiles] = high.reshape(PER // 16, 16, CW)
+                og[1, tiles] = (o - high.astype(F32)).astype(BF).reshape(PER // 16, 16, CW)
             return 0
-        lax.fori_loop(0, NE, body, 0)
+        lax.fori_loop(0, NE // 2, body, 0)
 
     def spread(s):
         total = None
@@ -228,18 +330,22 @@
             total = part if total is None else total + part
         return total
 
+    def spread_all(h, c, plus):
+        def body(j, _):
+            for n in range(4):
+                idx = (j, n // 2, n % 2, c, FULL, cols(h))
+                total = spread((j * 4 + n) * 2 + c)
+                if plus:
+                    total = total + x_all[idx].astype(F32)
+                x_all[idx] = total.astype(BF)
+            return 0
+        lax.fori_loop(0, 2, body, 0)
+
     def spread_other(h):
-        def body(j, _):
-            x_all[j // 4, (j // 2) % 2, j % 2, 1 - core, :, cols(h)] = spread(j * 2 + 1 - core).astype(BF)
-            return 0
-        lax.fori_loop(0, NDEV // 2, body, 0)
+        spread_all(h, 1 - core, False)
 
     def spread_mine(h):
-        def body(j, _):
-            idx = (j // 4, (j // 2) % 2, j % 2, core, FULL, cols(h))
-            x_all[idx] = (spread(j * 2 + core) + x_all[idx].astype(F32)).astype(BF)
-            return 0
-        lax.fori_loop(0, NDEV // 2, body, 0)
+        spread_all(h, core, True)
 
     def add_in(h, kind):
         for k in range(3):
@@ -311,32 +417,9 @@
     fin.wait()
 
 
-def route(ids, gates, ep_axes):
-    dense_g = []
-    for_all = jnp.arange(NDEV * NE)
-    match = ids[:, :, None] == for_all[None, None, :]
-    dense_g = jnp.sum(jnp.where(match, gates[:, :, None], 0.0), axis=1)
-    dense_m = jnp.any(match, axis=1).astype(F32)
-    both = jnp.stack([dense_g.T.reshape(NDEV, NE, TOK), dense_m.T.reshape(NDEV, NE, TOK)], axis=1)
-    got = lax.all_to_all(both, ep_axes, 0, 0, tiled=True)
-    gate, has = got[:, 0], got[:, 1] > 0.5
-    hit = jnp.any(has, axis=1)
-    slot = jnp.cumsum(hit.astype(jnp.int32), axis=1) - 1
-    l1 = (hit[:, None, :] & (slot[:, None, :] == jnp.arange(CAP)[None, :, None]))
-    within = jnp.cumsum(has.astype(jnp.int32), axis=2)
-    count = within[:, :, -1]
-    base = jnp.cumsum(count, axis=0) - count
-    rank = base[:, :, None] + within - 1
-    begin = jnp.minimum(base // 16 * 16, PER - WIN)
-    l1f = l1.astype(F32)
-    pick = lambda v: jnp.sum(jnp.where(l1[:, None, :, :], v[:, :, None, :], 0), axis=-1)
-    slot_rank = pick(jnp.where(has, rank + 1, 0)) - 1
-    l2 = slot_rank.transpose(1, 0, 2).reshape(NE, 1, SLOTS) == jnp.arange(PER)[None, :, None]
-    slot_gate = pick(gate).transpose(1, 0, 2).reshape(NE, 1, SLOTS)
-    gp = jnp.sum(jnp.where(l2, slot_gate, 0.0), axis=2).reshape(NE * PER, 1)
-    at = jnp.where(has, rank - begin[:, :, None], -1).transpose(0, 2, 1)
-    t = (at[:, :, :, None] == jnp.arange(WIN)[None, None, None, :]).reshape(NDEV, TOK, NE * WIN)
-    return l1.astype(BF), l2.reshape(NE * PER, SLOTS).astype(BF), t.astype(BF), gp, (begin // 16 + jnp.arange(NE)[None, :] * (PER // 16)).reshape(-1).astype(jnp.int32)
+def route(ids, gates):
+    match = ids.T[None, :, :] == jnp.arange(NDEV * NE)[:, None, None]
+    return jnp.sum(jnp.where(match, gates.T[None, :, :], 0.0), axis=1).reshape(NDEV, NE, TOK)
 
 
 def solution(mesh):
@@ -345,38 +428,50 @@
     vmem, anyspace = pl.BlockSpec(memory_space=pltpu.VMEM), pl.BlockSpec(memory_space=pl.ANY)
 
     def local_layer(tokens, ids, gates, w1, w3, w2):
-        l1, l2, t, gp, begin = route(ids, gates, ep_axes)
         return pl.pallas_call(
             layer_kernel,
             name="moe_layer",
             out_shape=jax.ShapeDtypeStruct((TOK, HID), BF),
-            in_specs=[anyspace] * 4 + [vmem] * 4 + [pl.BlockSpec(memory_space=pltpu.SMEM)],
+            in_specs=[anyspace, vmem, anyspace, anyspace, anyspace],
             out_specs=anyspace,
             scratch_shapes=[
                 pltpu.VMEM((2, 2, 2, 2, TOK, HID), BF),
                 pltpu.VMEM((NE * PER, FF), F32),
                 pltpu.VMEM((NE * PER, FF), F32),
                 pltpu.VMEM((NE * PER, FF), BF),
-                pltpu.VMEM((SLOTS, CW), BF),
                 pltpu.VMEM((2, NE * PER // 16, 16, CW), BF),
-                pltpu.VMEM((3, 2, CW, FF), BF),
-                pltpu.VMEM((3, FF, CW), BF),
+                pltpu.VMEM((2, 2, 2 * CW, FF), BF),
+                pltpu.VMEM((4, FF, CW), BF),
                 pltpu.VMEM((TOK, HID), BF),
                 pltpu.VMEM((2, 2, 2, TOK, CW), BF),
                 pltpu.VMEM((2, 2, TOK, CW), BF),
                 pltpu.VMEM((2, TOK, CW), BF),
+                pltpu.VMEM((NDEV, CAP, TOK), BF),
+                pltpu.VMEM((NE * PER, SLOTS), BF),
+                pltpu.VMEM((NDEV, TOK, NE * WIN), BF),
+                pltpu.VMEM((NE * PER, 1), F32),
+                pltpu.VMEM((NDEV, NE, TOK), F32),
+                pltpu.VMEM((NDEV * 8, TOK), F32),
+                pltpu.VMEM((NDEV * 8, TOK), F32),
+                pltpu.VMEM((NDEV * 8, TOK), F32),
+                pltpu.VMEM((NDEV, 4 * NE, TOK), BF),
+                pltpu.VMEM((8, SLOTS), F32),
+                pltpu.VMEM((TOK, 128), F32),
+                pltpu.SMEM((NDEV * NE,), jnp.int32),
                 pltpu.SemaphoreType.DMA((NC, 3, 5)),
                 pltpu.SemaphoreType.DMA((NC, 3, 5)),
                 pltpu.SemaphoreType.DMA((NC, 3, 3)),
                 pltpu.SemaphoreType.DMA((NC, 3, 3)),
                 pltpu.SemaphoreType.DMA((NC,)),
                 pltpu.SemaphoreType.DMA((NC,)),
-                pltpu.SemaphoreType.DMA((3, 2)),
-                pltpu.SemaphoreType.DMA((3,)),
+                pltpu.SemaphoreType.DMA((2, 2)),
+                pltpu.SemaphoreType.DMA((4,)),
                 pltpu.SemaphoreType.DMA((2,)),
+                pltpu.SemaphoreType.DMA((NDEV,)),
+                pltpu.SemaphoreType.DMA((NDEV,)),
                 pltpu.SemaphoreType.REGULAR,
             ],
             compiler_params=pltpu.CompilerParams(collective_id=0, has_side_effects=True, vmem_limit_bytes=67_043_328),
-        )(tokens, w1, w3, w2, l1, l2, t, gp, begin)
+        )(tokens, route(ids, gates), w1, w3, w2)
 
     return jax.shard_map(local_layer, mesh=mesh, in_specs=(row_spec, row_spec, row_spec, w_spec, w_spec, w_spec), out_specs=row_spec, check_vma=False)

time: 265 us -> 192 us (0.72)
  Pallas kernels: 209 us -> 187 us
  local copies, waits for them, and re-layouts: 23 us -> 2.95 us
  other arithmetic: 20.3 us -> 0.76 us
  waiting for transfers between devices: 5.95 us -> 0 us
  starting transfers between devices: 5.29 us -> 0 us
    pallas_call x1, Pallas kernels: 209 us -> 187 us  [local_layer(): pl.pallas_call(layer_kernel, name='moe_layer', out_shape=jax.ShapeDtypeSt...]
    eq x6 -> x0, local copies, waits for them, and re-layouts: 16.7 us -> none  [the longest x3 16.6 us: route(): at[:, :, :, None] == jnp.arange(WIN)[None, None, None, :]]
    convert_element_type x4 -> x0, other arithmetic: 9.59 us -> none  [the longest x1 6.59 us: route(): t.astype(BF)]
    all_to_all x1 -> x0, waiting for transfers between devices: 5.95 us -> none  [route(): got = lax.all_to_all(both, ep_axes, 0, 0, tiled=True)]
    all_to_all x1 -> x0, starting transfers between devices: 5.29 us -> none  [route(): got = lax.all_to_all(both, ep_axes, 0, 0, tiled=True)]
    reduce_sum x4 -> x1, other arithmetic: 4.43 us -> 0.76 us  [route(): jnp.sum(jnp.where(match, gates.T[None, :, :], 0.0), axis=1)]
    another operation x8 -> x0, other arithmetic: 3.07 us -> none
  transfers between devices with their start and end apart: 1 -> 0, of which waited for: 1 -> 0; matrix products, arithmetic and copies ran while one was open for 0% -> 0% of each run, Pallas kernels for 0% -> 0%
where the time goes in v2:
time: 192 us; the launch traced here: 191 us
  Pallas kernels  187 us (97%)
  local copies, waits for them, and re-layouts  2.95 us (2%)
    pallas_call x1, Pallas kernels, local_layer(): pl.pallas_call(layer_kernel, name='moe_layer', out_shape=jax.ShapeDtypeSt...  187 us

profile of v2, /device:TPU:0, one launch (start us, length us, event | category | flops | bytes accessed | tf_op | source)
XLA Modules:
  0.0 191.2 jit_solution(8231197997873496406)
XLA Ops:
  0.0 0.8 select_reduce_fusion
  0.8 0.7 reshape.5.meta_ref
  1.4 187.5 %moe_layer.1 = bf16[256,2048]{1,0:T(8,128)(2,1)} custom-call(bf16[256,2048]{1,0:T(8,128)(2,1)} %x_hbm.1, f32[16,4,256]{2,1,0:T(4,128)} %reshape.5.meta_ref, bf16[4,2048,1408]{2,1,0:T(8,128)(2,1)} %w1_hbm.1, bf16[4,2048,1408]{2,1,0:T(8,128)(2,1)} %w3_hbm.1, bf16[4,1408,2048]{2,1,0:T(8,128)(2,1)} %w2_hbm.1), custom_call_target="tpu_custom_call" | custom-call | tf_op jit(solution)/shard_map/moe_layer/pallas_call | solution.py:431
  188.9 2.3 %copy.8 = bf16[256,2048]{1,0:T(8,128)(2,1)} copy(bf16[256,2048]{1,0:T(8,128)(2,1)} %moe_layer.1) | data formatting | bytes 2097152

commit v3 on v2

--- a/solution.py
+++ b/solution.py
@@ -19,11 +19,11 @@
 
 
 def layer_kernel(x_hbm, meta_ref, w1_hbm, w3_hbm, w2_hbm, out_hbm,
-                 x_all, acc_a, acc_b, h_act, og, w13, w2b, xres, st0, st1, st2,
+                 x_all, acc_a, acc_b, h_act, og, w13, w2b, xres,
                  l1_ref, l2_ref, t_ref, gp_ref, meta, mrow, crow, at_rows, split, rslot, colq, st_ref,
                  ag_send, ag_recv, rs_send, rs_recv, d_send, d_recv, w13_sem, w2_sem, loc_sem, m_send, m_recv, credit):
-    slots = h_act.at[:, 2 * CW:3 * CW]
-    sgate = h_act.at[:, 3 * CW:3 * CW + 128]
+    slots = h_act.at[:, 2 * CW:4 * CW]
+    sgate = h_act.at[:, 4 * CW:4 * CW + 128]
     ez, ey, ex = lax.axis_index("ez"), lax.axis_index("ey"), lax.axis_index("ex")
     core = ex % 2
     pos = (ex // 2, ey, ez)
@@ -66,17 +66,17 @@
             ref, to = blocks(pick(k, tuple(a[:kind])), core, rows_of(k), h), nbr(a[kind])
         return pltpu.make_async_remote_copy(ref, ref, ag_send.at[h, k, kind], ag_recv.at[h, k, kind], device_id=to, device_id_type=MESH)
 
+    def landing(h, k, kind):
+        sel = [FULL] * 3
+        for i in range(kind + 1):
+            sel[(k + 2 - i) % 3] = 0 if i == kind else 1
+        return (sel[2], sel[1], sel[0], 1 - core, rows_of(k), cols((h + NC - 3) % NC))
+
     def rs(h, k, kind):
         a = [(k + 2 - i) % 3 for i in range(3)]
-        free = tuple(a[kind + 1:])
-        src = blocks(pick(k, free, (a[kind],)), core, rows_of(k), h)
-        if kind == 0:
-            dst = st0.at[h % 2, :, :, rows_of(k), :]
-        elif kind == 1:
-            dst = st1.at[h % 2, :, rows_of(k), :]
-        else:
-            dst = st2.at[h % 2, rows_of(k), :]
-        return pltpu.make_async_remote_copy(src, dst, rs_send.at[h, k, kind], rs_recv.at[h, k, kind], device_id=nbr(a[kind]), device_id_type=MESH)
+        src = blocks(pick(k, tuple(a[kind + 1:]), (a[kind],)), core, rows_of(k), h)
+        return pltpu.make_async_remote_copy(src, x_all.at[landing(h, k, kind)], rs_send.at[h, k, kind], rs_recv.at[h, k, kind],
+                                            device_id=nbr(a[kind]), device_id_type=MESH)
 
     def cross(h):
         ref = blocks((FULL, FULL, FULL), 1 - core, FULL, h)
@@ -89,7 +89,7 @@
 
     def w2_copy(i):
         e, h = i % NE, i // NE
-        return pltpu.make_async_copy(w2_hbm.at[e, :, cols(h)], w2b.at[i % 4], w2_sem.at[i % 4])
+        return pltpu.make_async_copy(w2_hbm.at[e, :, cols(h)], w2b.at[i % 6], w2_sem.at[i % 6])
 
     me = ez * 8 + ey * 4 + ex
 
@@ -127,6 +127,20 @@
         for k in range(3):
             ag(h, k, kind).wait_recv()
 
+    def service(h):
+        arrive(h, 1)
+        start(h, 2)
+        start(h, 3)
+
+        @pl.when(h + 2 < NC)
+        def _():
+            arrive(h + 2, 0)
+            start(h + 2, 1)
+
+        @pl.when(h + 4 < NC)
+        def _():
+            start(h + 4, 0)
+
     for h in range(4):
         start(h, 0)
 
@@ -155,6 +169,7 @@
         g2 = (g - g1).astype(BF).astype(F32)
         g3 = g - g1 - g2
         split[s] = jnp.concatenate([g1, g2, g3, jnp.zeros((4, TOK), F32)], axis=0).astype(BF)
+    service(0)
     c = mrow[...]
     lane = lax.broadcasted_iota(jnp.int32, c.shape, 1)
     for n in range(8):
@@ -208,17 +223,17 @@
         t_ref[s] = jnp.concatenate([jnp.where(q[:, e:e + 1] == place, 1.0, 0.0).astype(BF) for e in range(NE)], axis=1)
 
     def compact(h):
+        c = pl.ds(pl.multiple_of((h % 2) * CW, CW), CW)
         for s in range(NDEV):
             blk = x_all[s // 8, (s // 4) % 2, (s // 2) % 2, s % 2, :, cols(h)]
-            slots[s * CAP:(s + 1) * CAP, :] = jnp.dot(l1_ref[s], blk, preferred_element_type=F32).astype(BF)
-
-    def pack(h):
-        def body(n, _):
-            for e in range(2):
-                rows = pl.ds(pl.multiple_of((2 * n + e) * PER, PER), PER)
-                h_act[rows, pl.ds(pl.multiple_of((h % 2) * CW, CW), CW)] = jnp.dot(l2_ref[rows, :], slots[...], preferred_element_type=F32).astype(BF)
+            slots[s * CAP:(s + 1) * CAP, c] = jnp.dot(l1_ref[s], blk, preferred_element_type=F32).astype(BF)
+
+    def pack():
+        def body(e, _):
+            rows = pl.ds(pl.multiple_of(e * PER, PER), PER)
+            h_act[rows, :2 * CW] = jnp.dot(l2_ref[rows, :], slots[...], preferred_element_type=F32).astype(BF)
             return 0
-        lax.fori_loop(0, NE // 2, body, 0)
+        lax.fori_loop(0, NE, body, 0)
 
     def expert_in(g, e):
         i = g * NE + e
@@ -235,51 +250,37 @@
         acc_a[rows, :] += jnp.dot(xe, w13[i % 2, 0], preferred_element_type=F32)
         acc_b[rows, :] += jnp.dot(xe, w13[i % 2, 1], preferred_element_type=F32)
 
-    def experts_in(g):
+    def experts_in(g, lo, hi):
         def body(e, _):
             expert_in(g, e)
             return 0
-        lax.fori_loop(0, NE, body, 0)
+        lax.fori_loop(lo, hi, body, 0)
 
     def step_in(h, _):
-        @pl.when(h < NC)
-        def _():
-            arrive(h, 1)
-            start(h, 2)
-            start(h, 3)
-
-        @pl.when(h >= 1)
-        def _():
-            arrive(h - 1, 3)
-            arrive(h - 1, 4)
-            compact(h - 1)
-            pack(h - 1)
-
-        @pl.when(h + 2 < NC)
-        def _():
-            arrive(h + 2, 0)
-            start(h + 2, 1)
-
-        @pl.when(h + 4 < NC)
-        def _():
-            start(h + 4, 0)
-
-        @pl.when(jnp.logical_and(h >= 1, h % 2 == 0))
-        def _():
-            experts_in((h - 1) // 2)
-
-        @pl.when(h < NC)
-        def _():
-            fill_t(2 * h)
-            fill_t(2 * h + 1)
-
-        @pl.when(h < NC)
-        def _():
-            arrive(h, 2)
-            start(h, 4)
-        return 0
-
-    lax.fori_loop(0, NC + 1, step_in, 0)
+        arrive(h, 2)
+        start(h, 4)
+
+        @pl.when(h + 1 < NC)
+        def _():
+            service(h + 1)
+
+        @pl.when(jnp.logical_and(h % 2 == 0, h >= 2))
+        def _():
+            experts_in(h // 2 - 1, 2, NE)
+        fill_t(2 * h)
+        fill_t(2 * h + 1)
+        arrive(h, 3)
+        arrive(h, 4)
+        compact(h)
+
+        @pl.when(h % 2 == 1)
+        def _():
+            pack()
+            experts_in(h // 2, 0, 2)
+        return 0
+
+    lax.fori_loop(0, NC, step_in, 0)
+    experts_in(NC // 2 - 1, 2, NE)
     gate_rows()
 
     def drain(h, _):
@@ -290,8 +291,9 @@
     lax.fori_loop(0, NC, drain, 0)
     for i in range(1, NDEV):
         meta_copy(i).wait_send()
-    pl.semaphore_signal(credit, inc=1, device_id=partner, device_id_type=MESH)
-    for i in range(2):
+    for to in (nbr(0), nbr(1), nbr(2), partner):
+        pl.semaphore_signal(credit, inc=1, device_id=to, device_id_type=MESH)
+    for i in range(4):
         w2_copy(i).start()
 
     def activate(i, _):
@@ -308,13 +310,13 @@
             w2_copy(i).wait()
             w2_copy(i + 1).wait()
 
-            @pl.when(i + 2 < NC * NE)
+            @pl.when(i + 4 < NC * NE)
             def _():
-                w2_copy(i + 2).start()
-                w2_copy(i + 3).start()
+                w2_copy(i + 4).start()
+                w2_copy(i + 5).start()
             for e in range(2):
                 rows = pl.ds(pl.multiple_of((2 * n + e) * PER, PER), PER)
-                o = jnp.dot(h_act[rows, :], w2b[(i + e) % 4], preferred_element_type=F32) * gp_ref[rows, :]
+                o = jnp.dot(h_act[rows, :], w2b[(i + e) % 6], preferred_element_type=F32) * gp_ref[rows, :]
                 high = o.astype(BF)
                 tiles = pl.ds((2 * n + e) * (PER // 16), PER // 16)
                 og[0, tiles] = high.reshape(PER // 16, 16, CW)
@@ -350,23 +352,25 @@
     def add_in(h, kind):
         for k in range(3):
             rs(h, k, kind).wait_recv()
-            a = [(k + 2 - i) % 3 for i in range(3)]
-            free = a[kind + 1:]
             rows = rows_of(k)
-            if kind == 2:
-                sel = pos
-                mine = x_all[sel[2], sel[1], sel[0], core, rows, cols(h)].astype(F32) + st2[h % 2, rows, :].astype(F32)
-                xres[rows, cols(h)] = (xres[rows, cols(h)].astype(F32) + mine).astype(BF)
-                continue
-            order = sorted(free, reverse=True)
+            land = landing(h, k, kind)
+            order = [2 - i for i in range(3) if land[i] == FULL]
             for n in range(2 ** len(order)):
-                sel = list(pos)
-                bits = [(n >> (len(order) - 1 - b)) & 1 for b in range(len(order))]
-                for axis, bit in zip(order, bits):
+                sel, at = list(pos), list(land)
+                for b, axis in enumerate(order):
+                    bit = (n >> (len(order) - 1 - b)) & 1
                     sel[axis] = bit
-                got = st0[h % 2, bits[0], bits[1], rows, :] if kind == 0 else st1[h % 2, bits[0], rows, :]
+                    at[2 - axis] = bit
                 idx = (sel[2], sel[1], sel[0], core, rows, cols(h))
-                x_all[idx] = (x_all[idx].astype(F32) + got.astype(F32)).astype(BF)
+                total = x_all[idx].astype(F32) + x_all[tuple(at)].astype(F32)
+                if kind == 2:
+                    xres[rows, cols(h)] = (xres[rows, cols(h)].astype(F32) + total).astype(BF)
+                else:
+                    x_all[idx] = total.astype(BF)
+
+    def hop(h, kind):
+        for k in range(3):
+            rs(h, k, kind).start()
 
     def step_out(h, _):
         @pl.when(h < NC)
@@ -376,40 +380,40 @@
 
             @pl.when(h == 0)
             def _():
-                pl.semaphore_wait(credit, 1)
+                pl.semaphore_wait(credit, 4)
             cross(h).start()
 
-        @pl.when(jnp.logical_and(h >= 1, h < NC + 1))
-        def _():
-            add_in(h - 1, 0)
-            for k in range(3):
-                rs(h - 1, k, 1).start()
+        @pl.when(h >= 3)
+        def _():
+            add_in(h - 3, 2)
 
         @pl.when(h < NC)
         def _():
+            @pl.when(h >= 1)
+            def _():
+                cross(h - 1).wait_send()
             cross(h).wait_recv()
             spread_mine(h)
-            for k in range(3):
-                rs(h, k, 0).start()
+            hop(h, 0)
 
         @pl.when(jnp.logical_and(h >= 1, h < NC + 1))
         def _():
-            add_in(h - 1, 1)
-            for k in range(3):
-                rs(h - 1, k, 2).start()
-
-        @pl.when(h >= 2)
-        def _():
-            add_in(h - 2, 2)
-        return 0
-
-    lax.fori_loop(0, NC + 2, step_out, 0)
+            add_in(h - 1, 0)
+            hop(h - 1, 1)
+
+        @pl.when(jnp.logical_and(h >= 2, h < NC + 2))
+        def _():
+            add_in(h - 2, 1)
+            hop(h - 2, 2)
+        return 0
+
+    lax.fori_loop(0, NC + 3, step_out, 0)
+    cross(NC - 1).wait_send()
 
     def drain_out(h, _):
         for k in range(3):
             for kind in range(3):
                 rs(h, k, kind).wait_send()
-        cross(h).wait_send()
         return 0
     lax.fori_loop(0, NC, drain_out, 0)
     fin = pltpu.make_async_copy(xres, out_hbm, loc_sem.at[0])
@@ -441,11 +445,8 @@
                 pltpu.VMEM((NE * PER, FF), BF),
                 pltpu.VMEM((2, NE * PER // 16, 16, CW), BF),
                 pltpu.VMEM((2, 2, 2 * CW, FF), BF),
-                pltpu.VMEM((4, FF, CW), BF),
+                pltpu.VMEM((6, FF, CW), BF),
                 pltpu.VMEM((TOK, HID), BF),
-                pltpu.VMEM((2, 2, 2, TOK, CW), BF),
-                pltpu.VMEM((2, 2, TOK, CW), BF),
-                pltpu.VMEM((2, TOK, CW), BF),
                 pltpu.VMEM((NDEV, CAP, TOK), BF),
                 pltpu.VMEM((NE * PER, SLOTS), BF),
                 pltpu.VMEM((NDEV, TOK, NE * WIN), BF),
@@ -465,7 +466,7 @@
                 pltpu.SemaphoreType.DMA((NC,)),
                 pltpu.SemaphoreType.DMA((NC,)),
                 pltpu.SemaphoreType.DMA((2, 2)),
-                pltpu.SemaphoreType.DMA((4,)),
+                pltpu.SemaphoreType.DMA((6,)),
                 pltpu.SemaphoreType.DMA((2,)),
                 pltpu.SemaphoreType.DMA((NDEV,)),
                 pltpu.SemaphoreType.DMA((NDEV,)),

time: 192 us -> 183 us (0.953)
  Pallas kernels: 187 us -> 179 us
    pallas_call x1, Pallas kernels: 187 us -> 179 us  [local_layer(): pl.pallas_call(layer_kernel, name='moe_layer', out_shape=jax.ShapeDtypeSt...]
where the time goes in v3:
time: 183 us; the launch traced here: 182 us
  Pallas kernels  179 us (98%)
  local copies, waits for them, and re-layouts  2.95 us (2%)
    pallas_call x1, Pallas kernels, local_layer(): pl.pallas_call(layer_kernel, name='moe_layer', out_shape=jax.ShapeDtypeSt...  179 us

profile of v3, /device:TPU:0, one launch (start us, length us, event | category | flops | bytes accessed | tf_op | source)
XLA Modules:
  0.0 182.5 jit_solution(11040336110475729392)
XLA Ops:
  0.0 0.8 select_reduce_fusion
  0.8 0.7 reshape.5.meta_ref
  1.4 178.8 %moe_layer.1 = bf16[256,2048]{1,0:T(8,128)(2,1)} custom-call(bf16[256,2048]{1,0:T(8,128)(2,1)} %x_hbm.1, f32[16,4,256]{2,1,0:T(4,128)} %reshape.5.meta_ref, bf16[4,2048,1408]{2,1,0:T(8,128)(2,1)} %w1_hbm.1, bf16[4,2048,1408]{2,1,0:T(8,128)(2,1)} %w3_hbm.1, bf16[4,1408,2048]{2,1,0:T(8,128)(2,1)} %w2_hbm.1), custom_call_target="tpu_custom_call" | custom-call | tf_op jit(solution)/shard_map/moe_layer/pallas_call | solution.py:435
  180.2 2.3 %copy.8 = bf16[256,2048]{1,0:T(8,128)(2,1)} copy(bf16[256,2048]{1,0:T(8,128)(2,1)} %moe_layer.1) | data formatting | bytes 2097152
